TPU v7x, 32 devices: a whole 2x2x4 slice. The times are simulated.
32 devices in a mesh: kt: 8 (over z, y), tile: 4 (over x, core).
Axes of the slice: x: 2, y: 2, z: 4, core: 2. Of those that a mesh axis runs over, the one named last changes fastest.
Arguments:
- green_particle: bfloat16 [2, 64, 1024, 1024], P(None, 'kt', 'tile'), may hold values from -6 to 6
- green_hole: bfloat16 [2, 64, 1024, 1024], P(None, 'kt', 'tile'), may hold values from -6 to 6
- coulomb: bfloat16 [2, 64, 1024, 1024], P(None, 'kt'), may hold values from -3 to 3
Outputs:
- screened: float32 [2, 64, 1024, 1024], P(None, 'kt', 'tile')
All inputs are finite; a program needn't handle non-finite values.
Results may differ from a plain program's by a relative error of at most 0.0039.
Values may be sent and summed in bfloat16 or wider, within the bound.
No kernel may reach another device: no remote copies, remote signals or barrier semaphores. Data moves between devices by JAX's collectives and lax.ppermute only.
A program may use at most 192 MiB of HBM per device.

v0:
```python
import math
import jax
import jax.numpy as jnp
from jax import lax
from jax.sharding import PartitionSpec as P

KSIDE = 4
K = 64
HIGHEST = lax.Precision.HIGHEST


def phase_tables(points, side_count):
    point_index = jnp.arange(points, dtype=jnp.int32)
    digit_high = point_index // (side_count * side_count)
    digit_mid = point_index // side_count % side_count
    digit_low = point_index % side_count
    phase_turns = (
        digit_high[:, None] * digit_high[None, :]
        + digit_mid[:, None] * digit_mid[None, :]
        + digit_low[:, None] * digit_low[None, :]
    ) % side_count
    angles = phase_turns.astype(jnp.float32) * (2.0 * math.pi / side_count)
    return (jnp.cos(angles) / points, jnp.sin(angles) / points)


def to_cells(real_part, imag_part, cosine_table, sine_table):
    return (
        jnp.dot(cosine_table, real_part, precision=HIGHEST)
        - jnp.dot(sine_table, imag_part, precision=HIGHEST),
        jnp.dot(sine_table, real_part, precision=HIGHEST)
        + jnp.dot(cosine_table, imag_part, precision=HIGHEST),
    )


def to_momenta(real_part, imag_part, cosine_table, sine_table):
    return (
        jnp.dot(cosine_table, real_part, precision=HIGHEST)
        + jnp.dot(sine_table, imag_part, precision=HIGHEST),
        jnp.dot(cosine_table, imag_part, precision=HIGHEST)
        - jnp.dot(sine_table, real_part, precision=HIGHEST),
    )


def polarize(particle, hole_part):
    cosine_table, sine_table = phase_tables(K, KSIDE)
    part_real, part_imag = to_cells(
        particle[0].astype(jnp.float32), particle[1].astype(jnp.float32), cosine_table, sine_table
    )
    hole_real, hole_imag = to_cells(
        hole_part[0].astype(jnp.float32), hole_part[1].astype(jnp.float32), cosine_table, sine_table
    )
    cell_real = part_real * hole_real - part_imag * hole_imag
    cell_imag = part_real * hole_imag + part_imag * hole_real
    mom_real, mom_imag = to_momenta(cell_real, cell_imag, cosine_table, sine_table)
    return jnp.stack([mom_real, mom_imag]).astype(jnp.bfloat16)


def product_of(left_side, right_side):
    return jnp.einsum("kij,kjl->kil", left_side, right_side, preferred_element_type=jnp.float32)


def complex_batched(left_real, left_imag, right_real, right_imag):
    real_out = product_of(left_real, right_real) - product_of(left_imag, right_imag)
    imag_out = product_of(left_real, right_imag) + product_of(left_imag, right_real)
    return (real_out, imag_out)


def body(green_particle, green_hole, coulomb):
    tile_rows = green_particle.shape[2]
    moved_part, moved_hole = (
        lax.all_to_all(green_particle, "kt", split_axis=3, concat_axis=1, tiled=True),
        lax.all_to_all(green_hole, "kt", split_axis=3, concat_axis=1, tiled=True),
    )
    points = moved_part.shape[1]
    narrow = moved_part.shape[3]
    polar_q = polarize(
        moved_part.reshape(2, points, tile_rows * narrow),
        moved_hole.reshape(2, points, tile_rows * narrow),
    )
    polar_q = polar_q.reshape(2, points, tile_rows, narrow)
    polar_rows = lax.all_to_all(polar_q, "kt", split_axis=1, concat_axis=3, tiled=True)
    mid_real, mid_imag = complex_batched(polar_rows[0], polar_rows[1], coulomb[0], coulomb[1])
    mid_stack = jnp.stack([mid_real.astype(jnp.bfloat16), mid_imag.astype(jnp.bfloat16)])
    row_start = lax.axis_index("tile") * tile_rows
    coulomb_rows = lax.dynamic_slice_in_dim(coulomb, row_start, tile_rows, 2)
    segment = lax.all_gather(mid_stack, "tile", axis=2, tiled=True)
    left_real = coulomb_rows[0]
    left_imag = coulomb_rows[1]
    more_real, more_imag = complex_batched(left_real, left_imag, segment[0], segment[1])
    summed = jnp.stack([more_real, more_imag])
    return coulomb_rows.astype(jnp.float32) + summed


def solution(mesh):
    return jax.shard_map(
        body,
        mesh=mesh,
        in_specs=(
            P(None, "kt", "tile", None),
            P(None, "kt", "tile", None),
            P(None, "kt", None, None),
        ),
        out_specs=P(None, "kt", "tile", None),
        check_vma=False,
    )
```

profile of v0, /device:TPU:0, one launch (start us, length us, event | category | flops | bytes accessed | tf_op | source)
XLA Modules:
  0.0 1116.9 jit_solution(6014429570869471573)
XLA Ops:
  6.5 12.6 %copy.8 = bf16[2,8,256,1024]{2,1,0,3:T(8,128)(2,1)} copy(bf16[2,8,256,1024]{3,2,1,0:T(8,128)(2,1)} %param.3) | data formatting | bytes 16777216 | tf_op args[0]
  19.1 7.3 all-to-all-start
  26.4 12.5 %copy.10 = bf16[2,8,256,1024]{2,1,0,3:T(8,128)(2,1)} copy(bf16[2,8,256,1024]{3,2,1,0:T(8,128)(2,1)} %param.4) | data formatting | bytes 16777216 | tf_op args[1]
  38.9 170.7 %all-to-all-done = bf16[2,8,256,1024]{2,1,0,3:T(8,128)(2,1)} async-done(((bf16[2,8,256,1024]{2,1,0,3:T(8,128)(2,1)}), bf16[2,8,256,1024]{2,1,0,3:T(8,128)(2,1)}, u32[]{:S(2)}, u32[]{:S(2)}) %all-to-all-start) | async-done | bytes 8388640 | tf_op jit(solution)/shard_map/all_to_all | solution.py:71
  209.6 5.0 all-to-all-start.1
  214.6 0.0 all-gather.2.cloned.1.call-start
  214.7 12.5 %copy.9 = bf16[2,8,256,8,128]{4,2,1,3,0:T(8,128)(2,1)} copy(bf16[2,8,256,8,128]{2,1,0,4,3:T(8,128)(2,1)} %bitcast.1) | data formatting | bytes 16777216 | tf_op jit(solution)/shard_map/all_to_all | solution.py:71
  227.2 5.3 slice_bitcast_fusion.8
  232.5 14.0 %fusion.28 = f32[64,32768]{1,0:T(8,128)} fusion(bf16[8,8,256,128]{3,2,1,0:T(8,128)(2,1)S(1)} %get-tuple-element.12, s32[64]{0:T(128)S(1)} %get-tuple-element.13, s32[64]{0:T(128)S(1)} %get-tuple-element.14, s32[64]{0:T(128)S(1)} %and_select_fusion.3), kind=kOutput, calls=%fused_computation.48 | convolution fusion | flops 1610690560 | bytes 12583680 | tf_op jit(solution)/shard_map/dot_general | solution.py:30
  246.5 14.5 %fusion.30 = f32[64,32768]{1,0:T(8,128)} fusion(bf16[8,8,256,128]{3,2,1,0:T(8,128)(2,1)S(1)} %get-tuple-element.12, s32[64]{0:T(128)S(1)} %get-tuple-element.13, s32[64]{0:T(128)S(1)} %get-tuple-element.14, s32[64]{0:T(128)S(1)} %and_select_fusion.3), kind=kOutput, calls=%fused_computation.50 | convolution fusion | flops 1610690560 | bytes 12583680 | tf_op jit(solution)/shard_map/dot_general | solution.py:28
  261.0 135.8 %all-to-all-done.1 = bf16[2,8,256,1024]{2,1,0,3:T(8,128)(2,1)} async-done(((bf16[2,8,256,1024]{2,1,0,3:T(8,128)(2,1)}), bf16[2,8,256,1024]{2,1,0,3:T(8,128)(2,1)}, u32[]{:S(2)}, u32[]{:S(2)}) %all-to-all-start.1) | async-done | bytes 8388640 | tf_op jit(solution)/shard_map/all_to_all | solution.py:72
  396.9 12.2 %copy.11 = bf16[2,8,256,8,128]{4,2,1,3,0:T(8,128)(2,1)} copy(bf16[2,8,256,8,128]{2,1,0,4,3:T(8,128)(2,1)} %bitcast.3) | data formatting | bytes 16777216 | tf_op jit(solution)/shard_map/all_to_all | solution.py:72
  409.1 4.0 slice_bitcast_fusion.6
  413.1 5.4 fusion.22
  418.4 5.4 fusion.24
  423.9 0.0 slice-start.2
  423.9 14.6 %convolution_add_fusion = f32[64,32768]{1,0:T(8,128)} fusion(f32[64,32768]{1,0:T(8,128)S(1)} %fusion.22, bf16[8,8,256,128]{3,2,1,0:T(8,128)(2,1)S(1)} %get-tuple-element.9, s32[64]{0:T(128)S(1)} %get-tuple-element.13, s32[64]{0:T(128)S(1)} %get-tuple-element.14, s32[64]{0:T(128)S(1)} %and_select_fusion.3), kind=kOutput, calls=%fused_computation | convolution fusion | flops 1612787712 | bytes 20972288 | tf_op jit(solution)/shard_map/dot_general | solution.py:31
  438.5 14.7 %convolution_subtract_fusion = f32[64,32768]{1,0:T(8,128)} fusion(f32[64,32768]{1,0:T(8,128)S(1)} %fusion.24, bf16[8,8,256,128]{3,2,1,0:T(8,128)(2,1)S(1)} %get-tuple-element.9, s32[64]{0:T(128)S(1)} %get-tuple-element.13, s32[64]{0:T(128)S(1)} %get-tuple-element.14, s32[64]{0:T(128)S(1)} %and_select_fusion.3), kind=kOutput, calls=%fused_computation.2 | convolution fusion | flops 1612787712 | bytes 20972288 | tf_op jit(solution)/shard_map/dot_general | solution.py:29
  453.3 14.4 %convolution_subtract_fusion.1 = f32[64,32768]{1,0:T(8,128)} fusion(f32[64,32768]{1,0:T(8,128)S(1)} %bitcast.119, bf16[8,8,256,128]{3,2,1,0:T(8,128)(2,1)S(1)} %copy-done.1, s32[64]{0:T(128)S(1)} %get-tuple-element.13, s32[64]{0:T(128)S(1)} %get-tuple-element.14, s32[64]{0:T(128)S(1)} %and_select_fusion.3), kind=kOutput, calls=%fused_computation.3 | convolution fusion | flops 1612787712 | bytes 20972288 | tf_op jit(solution)/shard_map/dot_general | solution.py:29
  467.7 22.5 %multiply_subtract_fusion = (f32[64,32768]{1,0:T(8,128)}, f32[64,32768]{1,0:T(8,128)}) fusion(f32[64,32768]{1,0:T(8,128)} %convolution_add_fusion, f32[64,32768]{1,0:T(8,128)} %convolution_subtract_fusion.1, f32[64,32768]{1,0:T(8,128)} %convolution_subtract_fusion, f32[64,32768]{1,0:T(8,128)} %fusion.28, bf16[8,8,256,128]{3,2,1,0:T(8,128)(2,1)} %get-tuple-element.11, ...), kind=kOutput, calls=%fused_computation.35 | convolution fusion | flops 1625370624 | bytes 54526720 | tf_op jit(solution)/shard_map/dot_general | solution.py:31
  490.2 12.3 %fusion.50 = f32[64,32768]{1,0:T(8,128)} fusion(f32[64,32768]{1,0:T(8,128)} %get-tuple-element.5, s32[64]{0:T(128)S(1)} %get-tuple-element.13, s32[64]{0:T(128)S(1)} %get-tuple-element.14, s32[64]{0:T(128)S(1)} %and_select_fusion.3), kind=kOutput, calls=%fused_computation.77 | convolution fusion | flops 1610690560 | bytes 16777984 | tf_op jit(solution)/shard_map/dot_general | solution.py:37
  502.6 7.8 fusion.49
  510.3 0.0 slice-start.1
  510.3 12.9 %fusion.45 = bf16[8,8,256,128]{3,1,2,0:T(8,128)(2,1)} fusion(f32[64,32768]{1,0:T(8,128)} %fusion.50, f32[64,32768]{1,0:T(8,128)S(1)} %copy-done, s32[64]{0:T(128)S(1)} %get-tuple-element.13, s32[64]{0:T(128)S(1)} %get-tuple-element.14, s32[64]{0:T(128)S(1)} %and_select_fusion.3), kind=kOutput, calls=%fused_computation.67 | convolution fusion | flops 1614884864 | bytes 20972288 | tf_op jit(solution)/shard_map/dot_general | solution.py:38
  523.3 8.9 fusion.44
  532.2 1.2 copy.20
  533.3 0.5 bitcast_bitcast_fusion
  533.8 0.5 copy-done.2
  534.3 1.2 copy.19
  535.5 2.2 bitcast_bitcast_fusion.1
  537.7 6.4 pad_maximum_fusion
  544.1 187.9 %all_to_all.45 = bf16[2,64,256,128]{3,2,0,1:T(8,128)(2,1)} all-to-all(bf16[2,64,256,128]{3,2,0,1:T(8,128)(2,1)} %pad_maximum_fusion), channel_id=1, replica_groups=mesh['kt'=8,'tile'=4] {'kt'}, dimensions={1} | all-to-all | bytes 16777216 | tf_op jit(solution)/shard_map/all_to_all | solution.py:81
  732.0 13.9 %copy.56 = bf16[2,8,8,256,128]{4,1,3,2,0:T(8,128)(2,1)} copy(bf16[2,8,8,256,128]{4,3,0,2,1:T(8,128)(2,1)} %bitcast.123) | data formatting | bytes 16777216 | tf_op jit(solution)/shard_map/all_to_all | solution.py:81
  745.9 5.8 fusion.116
  751.6 7.3 squeeze.43
  759.0 7.4 squeeze.41
  766.4 15.1 %fusion.2 = f32[8,256,1024]{2,1,0:T(8,128)} fusion(bf16[8,256,1024]{2,1,0:T(8,128)(2,1)} %squeeze.41, bf16[2,8,1024,1024]{3,2,1,0:T(8,128)(2,1)} %param.5), kind=kOutput, calls=%fused_computation.11 | convolution fusion | flops 4294967296 | bytes 29360128 | tf_op jit(solution)/shard_map/kij,kjl->kil/dot_general | solution.py:59
  781.5 13.6 %fusion.4 = f32[8,256,1024]{2,1,0:T(8,128)} fusion(bf16[8,256,1024]{2,1,0:T(8,128)(2,1)S(1)} %copy-done.3, bf16[2,8,1024,1024]{3,2,1,0:T(8,128)(2,1)} %param.5), kind=kOutput, calls=%fused_computation.13 | convolution fusion | flops 4294967296 | bytes 29360128 | tf_op jit(solution)/shard_map/kij,kjl->kil/dot_general | solution.py:59
  795.1 14.8 %fusion.19 = bf16[1,8,256,1024]{3,2,1,0:T(8,128)(2,1)} fusion(f32[8,256,1024]{2,1,0:T(8,128)} %fusion.2, bf16[8,256,1024]{2,1,0:T(8,128)(2,1)S(1)} %copy-done.3, bf16[2,8,1024,1024]{3,2,1,0:T(8,128)(2,1)} %param.5), kind=kOutput, calls=%fused_computation.37 | convolution fusion | flops 4299161600 | bytes 33554432 | tf_op jit(solution)/shard_map/kij,kjl->kil/dot_general | solution.py:59
  809.9 13.7 %fusion.18 = bf16[1,8,256,1024]{3,2,1,0:T(8,128)(2,1)} fusion(f32[8,256,1024]{2,1,0:T(8,128)} %fusion.4, bf16[8,256,1024]{2,1,0:T(8,128)(2,1)} %squeeze.41, bf16[2,8,1024,1024]{3,2,1,0:T(8,128)(2,1)} %param.5), kind=kOutput, calls=%fused_computation.36 | convolution fusion | flops 4299161600 | bytes 33554432 | tf_op jit(solution)/shard_map/kij,kjl->kil/dot_general | solution.py:59
  823.6 6.4 pad_maximum_fusion.1
  830.0 0.0 all-gather.2.cloned.1.call-update
  830.0 200.5 %all-gather.2.cloned.1.call-done = bf16[2,8,1024,1024]{3,2,1,0:T(8,128)(2,1)} async-done(((bf16[2,8,256,1024]{3,2,1,0:T(8,128)(2,1)}), bf16[2,8,1024,1024]{3,2,1,0:T(8,128)(2,1)}) %all-gather.2.cloned.1.call-update) | async-done | bytes 33554448 | tf_op jit(solution)/shard_map/all_gather | solution.py:86
  1030.5 14.8 %fusion.11 = f32[8,256,1024]{2,1,0:T(8,128)} fusion(bf16[2,8,1024,1024]{3,2,1,0:T(8,128)(2,1)} %all-gather.2.cloned.1.call-done, bf16[2,8,1024,1024]{3,2,1,0:T(8,128)(2,1)} %param.5, s32[]{:T(128)S(6)} %select_n.170), kind=kOutput, calls=%fused_computation.20 | convolution fusion | flops 4294967296 | bytes 29360132 | tf_op jit(solution)/shard_map/kij,kjl->kil/dot_general | solution.py:59
  1045.3 15.0 %fusion.10 = f32[8,256,1024]{2,1,0:T(8,128)} fusion(bf16[2,8,1024,1024]{3,2,1,0:T(8,128)(2,1)} %all-gather.2.cloned.1.call-done, bf16[2,8,1024,1024]{3,2,1,0:T(8,128)(2,1)} %param.5, s32[]{:T(128)S(6)} %add.203, s32[]{:T(128)S(6)} %select_n.170), kind=kOutput, calls=%fused_computation.19 | convolution fusion | flops 4294967296 | bytes 29360136 | tf_op jit(solution)/shard_map/kij,kjl->kil/dot_general | solution.py:59
  1060.3 17.2 %add_bitcast_fusion = f32[1,8,256,1024]{3,2,1,0:T(8,128)} fusion(f32[8,256,1024]{2,1,0:T(8,128)} %fusion.10, bf16[2,8,1024,1024]{3,2,1,0:T(8,128)(2,1)} %all-gather.2.cloned.1.call-done, bf16[2,8,1024,1024]{3,2,1,0:T(8,128)(2,1)} %param.5, s32[]{:T(128)S(6)} %select_n.170), kind=kOutput, calls=%fused_computation.30 | convolution fusion | flops 4297064448 | bytes 37748740 | tf_op jit(solution)/shard_map/kij,kjl->kil/dot_general | solution.py:59
  1077.5 17.5 %subtract_bitcast_fusion = f32[1,8,256,1024]{3,2,1,0:T(8,128)} fusion(f32[8,256,1024]{2,1,0:T(8,128)} %fusion.11, bf16[2,8,1024,1024]{3,2,1,0:T(8,128)(2,1)} %all-gather.2.cloned.1.call-done, bf16[2,8,1024,1024]{3,2,1,0:T(8,128)(2,1)} %param.5, s32[]{:T(128)S(6)} %add.203, s32[]{:T(128)S(6)} %select_n.170), kind=kOutput, calls=%fused_computation.31 | convolution fusion | flops 4297064448 | bytes 37748744 | tf_op jit(solution)/shard_map/kij,kjl->kil/dot_general | solution.py:59
  1095.0 14.7 %maximum_add_fusion = f32[2,8,256,1024]{3,2,1,0:T(8,128)} fusion(f32[1,8,256,1024]{3,2,1,0:T(8,128)} %add_bitcast_fusion, f32[1,8,256,1024]{3,2,1,0:T(8,128)} %subtract_bitcast_fusion, bf16[2,8,1024,1024]{3,2,1,0:T(8,128)(2,1)} %param.5, s32[]{:T(128)S(6)} %select_n.170), kind=kLoop, calls=%fused_computation.10 | loop fusion | flops 12582912 | bytes 41943044 | tf_op jit(solution)/shard_map/add | solution.py:91
  (19 shorter events, 0.0 us)
Async XLA Ops:
  19.1 190.5 %all-to-all-start = ((bf16[2,8,256,1024]{2,1,0,3:T(8,128)(2,1)}), bf16[2,8,256,1024]{2,1,0,3:T(8,128)(2,1)}, u32[]{:S(2)}, u32[]{:S(2)}) async-start(bf16[2,8,256,1024]{2,1,0,3:T(8,128)(2,1)} %copy.8), calls=%async_computation | async-start | bytes 16777216 | tf_op jit(solution)/shard_map/all_to_all | solution.py:71
  209.6 187.3 %all-to-all-start.1 = ((bf16[2,8,256,1024]{2,1,0,3:T(8,128)(2,1)}), bf16[2,8,256,1024]{2,1,0,3:T(8,128)(2,1)}, u32[]{:S(2)}, u32[]{:S(2)}) async-start(bf16[2,8,256,1024]{2,1,0,3:T(8,128)(2,1)} %copy.10), calls=%async_computation.1 | async-start | bytes 16777216 | tf_op jit(solution)/shard_map/all_to_all | solution.py:72
  214.6 815.9 %all-gather.2.cloned.1.call-start = ((), (), s32[]{:S(2)}) async-start(), calls=%async_computation.3 | async-start | bytes 41943040 | tf_op jit(solution)/shard_map/all_gather | solution.py:86
  423.9 29.4 %slice-start.2 = ((s8[8388608]{0:T(1024)(128)(4,1)}), s8[4194304]{0:T(1024)(128)(4,1)S(1)}, s32[]{:S(2)}) async-start(s8[8388608]{0:T(1024)(128)(4,1)} %bitcast.118), calls=%async_computation.6 | async-start | bytes 8388608
  438.5 14.8 %copy-start.1 = (bf16[8,8,256,128]{3,2,1,0:T(8,128)(2,1)S(1)}, bf16[8,8,256,128]{3,2,1,0:T(8,128)(2,1)}, u32[]{:S(2)}) copy-start(bf16[8,8,256,128]{3,2,1,0:T(8,128)(2,1)} %get-tuple-element.11) | copy-start | bytes 12582916
  438.5 14.8 %slice-start.3 = ((s8[8388608]{0:T(1024)(128)(4,1)}), s8[4194304]{0:T(1024)(128)(4,1)S(1)}, s32[]{:S(2)}) async-start(s8[8388608]{0:T(1024)(128)(4,1)} %bitcast.118), calls=%async_computation.7 | async-start | bytes 8388608
  490.2 12.3 %copy-start = (f32[64,32768]{1,0:T(8,128)S(1)}, f32[64,32768]{1,0:T(8,128)}, u32[]{:S(2)}) copy-start(f32[64,32768]{1,0:T(8,128)} %get-tuple-element.6) | copy-start | bytes 25165828
  502.5 20.7 %slice-start = ((s8[8388608]{0:T(1024)(128)(4,1)}), s8[4194304]{0:T(1024)(128)(4,1)S(1)}, s32[]{:S(2)}) async-start(s8[8388608]{0:T(1024)(128)(4,1)} %bitcast.116), calls=%async_computation.4 | async-start | bytes 8388608
  510.3 12.9 %slice-start.1 = ((s8[8388608]{0:T(1024)(128)(4,1)}), s8[4194304]{0:T(1024)(128)(4,1)S(1)}, s32[]{:S(2)}) async-start(s8[8388608]{0:T(1024)(128)(4,1)} %bitcast.116), calls=%async_computation.5 | async-start | bytes 8388608
  532.1 2.2 copy-start.2
  766.4 15.1 %copy-start.3 = (bf16[8,256,1024]{2,1,0:T(8,128)(2,1)S(1)}, bf16[8,256,1024]{2,1,0:T(8,128)(2,1)}, u32[]{:S(2)}) copy-start(bf16[8,256,1024]{2,1,0:T(8,128)(2,1)} %squeeze.43) | copy-start | bytes 12582916
  809.9 13.8 %copy-start.4 = (bf16[1,8,256,1024]{3,2,1,0:T(8,128)(2,1)S(1)}, bf16[1,8,256,1024]{3,2,1,0:T(8,128)(2,1)}, u32[]{:S(2)}) copy-start(bf16[1,8,256,1024]{3,2,1,0:T(8,128)(2,1)} %fusion.19) | copy-start | bytes 12582916
Sparse Core Ops, SparseCore 0:
  830.1 200.3 all-gather.1
where the time goes:
time: 1120 us
  waiting for transfers between devices  507 us (45%)
  matrix products  269 us (24%)
  blocking collectives  188 us (17%)
  local copies, waits for them, and re-layouts  99 us (9%)
  other arithmetic  27.4 us (2%)
  between operations  14 us (1%)
  starting transfers between devices  12.4 us (1%)
    all_gather x1, waiting for transfers between devices, body(): segment = lax.all_gather(mid_stack, 'tile', axis=2, tiled=True)  201 us
    all_to_all x1, blocking collectives, body(): lax.all_to_all(polar_q, 'kt', split_axis=1, concat_axis=3, tiled=True)  188 us
    all_to_all x1, waiting for transfers between devices, body(): lax.all_to_all(green_particle, 'kt', split_axis=3, concat_axis=1, tiled=T...  171 us
    all_to_all x1, waiting for transfers between devices, body(): lax.all_to_all(green_hole, 'kt', split_axis=3, concat_axis=1, tiled=True)  136 us
    dot_general x8, matrix products, product_of(): jnp.einsum('kij,kjl->kil', left_side, right_side, preferred_element_type=...  122 us
    unnamed x24, local copies, waits for them, and re-layouts  37.2 us
    dot_general x2, matrix products, to_cells(): jnp.dot(cosine_table, imag_part, precision=HIGHEST)  37.1 us
    dot_general x2, matrix products, to_cells(): jnp.dot(sine_table, imag_part, precision=HIGHEST)  29.1 us
  transfers between devices with their start and end apart: 3, of which 3 were waited for; matrix products, arithmetic and copies ran while one was open for 5% of the time, Pallas kernels for 0%

commit v1 on v0

--- a/solution.py
+++ b/solution.py
@@ -78,7 +78,10 @@
         moved_hole.reshape(2, points, tile_rows * narrow),
     )
     polar_q = polar_q.reshape(2, points, tile_rows, narrow)
-    polar_rows = lax.all_to_all(polar_q, "kt", split_axis=1, concat_axis=3, tiled=True)
+    size = lax.axis_size("kt")
+    parts = jnp.stack(jnp.split(polar_q, size, axis=1), axis=0)
+    parts = lax.all_to_all(parts, "kt", split_axis=0, concat_axis=0)
+    polar_rows = jnp.concatenate(parts, axis=3)
     mid_real, mid_imag = complex_batched(polar_rows[0], polar_rows[1], coulomb[0], coulomb[1])
     mid_stack = jnp.stack([mid_real.astype(jnp.bfloat16), mid_imag.astype(jnp.bfloat16)])
     row_start = lax.axis_index("tile") * tile_rows

time: 1120 us -> 1120 us (level)
    all_to_all x1 -> x0, local copies, waits for them, and re-layouts: 13.9 us -> none  [body(): lax.all_to_all(polar_q, 'kt', split_axis=1, concat_axis=3, tiled=True)]
    unnamed x24 -> x32, local copies, waits for them, and re-layouts: 37.2 us -> 40.4 us
where the time goes in v1:
time: 1120 us; the launch traced here: 1110 us
  waiting for transfers between devices  507 us (45%)
  matrix products  271 us (24%)
  blocking collectives  187 us (17%)
  local copies, waits for them, and re-layouts  94.8 us (8%)
  other arithmetic  21 us (2%)
  between operations  14.1 us (1%)
  starting transfers between devices  12.4 us (1%)
    all_gather x1, waiting for transfers between devices, body(): segment = lax.all_gather(mid_stack, 'tile', axis=2, tiled=True)  201 us
    all_to_all x1, blocking collectives, body(): parts = lax.all_to_all(parts, 'kt', split_axis=0, concat_axis=0)  187 us
    all_to_all x1, waiting for transfers between devices, body(): lax.all_to_all(green_particle, 'kt', split_axis=3, concat_axis=1, tiled=T...  171 us
    all_to_all x1, waiting for transfers between devices, body(): lax.all_to_all(green_hole, 'kt', split_axis=3, concat_axis=1, tiled=True)  136 us
    dot_general x8, matrix products, product_of(): jnp.einsum('kij,kjl->kil', left_side, right_side, preferred_element_type=...  122 us
    unnamed x32, local copies, waits for them, and re-layouts  40.4 us
    dot_general x2, matrix products, to_cells(): jnp.dot(cosine_table, imag_part, precision=HIGHEST)  37.1 us
    dot_general x2, matrix products, to_cells(): jnp.dot(sine_table, imag_part, precision=HIGHEST)  29.2 us
  transfers between devices with their start and end apart: 3, of which 3 were waited for; matrix products, arithmetic and copies ran while one was open for 5% of the time, Pallas kernels for 0%

profile of v1, /device:TPU:0, one launch (start us, length us, event | category | flops | bytes accessed | tf_op | source)
XLA Modules:
  0.0 1107.2 jit_solution(12600023614240701714)
XLA Ops:
  6.5 12.6 %copy.10 = bf16[2,8,256,1024]{2,1,0,3:T(8,128)(2,1)} copy(bf16[2,8,256,1024]{3,2,1,0:T(8,128)(2,1)} %param.3) | data formatting | bytes 16777216 | tf_op args[0]
  19.1 7.3 all-to-all-start
  26.4 12.5 %copy.12 = bf16[2,8,256,1024]{2,1,0,3:T(8,128)(2,1)} copy(bf16[2,8,256,1024]{3,2,1,0:T(8,128)(2,1)} %param.4) | data formatting | bytes 16777216 | tf_op args[1]
  38.9 170.7 %all-to-all-done = bf16[2,8,256,1024]{2,1,0,3:T(8,128)(2,1)} async-done(((bf16[2,8,256,1024]{2,1,0,3:T(8,128)(2,1)}), bf16[2,8,256,1024]{2,1,0,3:T(8,128)(2,1)}, u32[]{:S(2)}, u32[]{:S(2)}) %all-to-all-start) | async-done | bytes 8388640 | tf_op jit(solution)/shard_map/all_to_all | solution.py:71
  209.6 5.0 all-to-all-start.1
  214.7 12.5 %copy.11 = bf16[2,8,256,8,128]{4,2,1,3,0:T(8,128)(2,1)} copy(bf16[2,8,256,8,128]{2,1,0,4,3:T(8,128)(2,1)} %bitcast.1) | data formatting | bytes 16777216 | tf_op jit(solution)/shard_map/all_to_all | solution.py:71
  227.2 5.3 slice_bitcast_fusion.8
  232.5 14.0 %fusion.28 = f32[64,32768]{1,0:T(8,128)} fusion(bf16[8,8,256,128]{3,2,1,0:T(8,128)(2,1)S(1)} %get-tuple-element.12, s32[64]{0:T(128)S(1)} %get-tuple-element.13, s32[64]{0:T(128)S(1)} %get-tuple-element.14, s32[64]{0:T(128)S(1)} %and_select_fusion.3), kind=kOutput, calls=%fused_computation.46 | convolution fusion | flops 1610690560 | bytes 12583680 | tf_op jit(solution)/shard_map/dot_general | solution.py:30
  246.5 14.5 %fusion.30 = f32[64,32768]{1,0:T(8,128)} fusion(bf16[8,8,256,128]{3,2,1,0:T(8,128)(2,1)S(1)} %get-tuple-element.12, s32[64]{0:T(128)S(1)} %get-tuple-element.13, s32[64]{0:T(128)S(1)} %get-tuple-element.14, s32[64]{0:T(128)S(1)} %and_select_fusion.3), kind=kOutput, calls=%fused_computation.48 | convolution fusion | flops 1610690560 | bytes 12583680 | tf_op jit(solution)/shard_map/dot_general | solution.py:28
  261.0 135.8 %all-to-all-done.1 = bf16[2,8,256,1024]{2,1,0,3:T(8,128)(2,1)} async-done(((bf16[2,8,256,1024]{2,1,0,3:T(8,128)(2,1)}), bf16[2,8,256,1024]{2,1,0,3:T(8,128)(2,1)}, u32[]{:S(2)}, u32[]{:S(2)}) %all-to-all-start.1) | async-done | bytes 8388640 | tf_op jit(solution)/shard_map/all_to_all | solution.py:72
  396.9 12.2 %copy.13 = bf16[2,8,256,8,128]{4,2,1,3,0:T(8,128)(2,1)} copy(bf16[2,8,256,8,128]{2,1,0,4,3:T(8,128)(2,1)} %bitcast.3) | data formatting | bytes 16777216 | tf_op jit(solution)/shard_map/all_to_all | solution.py:72
  409.1 4.0 slice_bitcast_fusion.6
  413.1 5.4 fusion.22
  418.4 5.4 fusion.24
  423.9 14.6 %convolution_add_fusion = f32[64,32768]{1,0:T(8,128)} fusion(f32[64,32768]{1,0:T(8,128)S(1)} %fusion.22, bf16[8,8,256,128]{3,2,1,0:T(8,128)(2,1)S(1)} %get-tuple-element.9, s32[64]{0:T(128)S(1)} %get-tuple-element.13, s32[64]{0:T(128)S(1)} %get-tuple-element.14, s32[64]{0:T(128)S(1)} %and_select_fusion.3), kind=kOutput, calls=%fused_computation | convolution fusion | flops 1612787712 | bytes 20972288 | tf_op jit(solution)/shard_map/dot_general | solution.py:31
  438.4 14.8 %convolution_subtract_fusion = f32[64,32768]{1,0:T(8,128)} fusion(f32[64,32768]{1,0:T(8,128)S(1)} %fusion.24, bf16[8,8,256,128]{3,2,1,0:T(8,128)(2,1)S(1)} %get-tuple-element.9, s32[64]{0:T(128)S(1)} %get-tuple-element.13, s32[64]{0:T(128)S(1)} %get-tuple-element.14, s32[64]{0:T(128)S(1)} %and_select_fusion.3), kind=kOutput, calls=%fused_computation.2 | convolution fusion | flops 1612787712 | bytes 20972288 | tf_op jit(solution)/shard_map/dot_general | solution.py:29
  453.3 14.4 %convolution_subtract_fusion.1 = f32[64,32768]{1,0:T(8,128)} fusion(f32[64,32768]{1,0:T(8,128)S(1)} %bitcast.144, bf16[8,8,256,128]{3,2,1,0:T(8,128)(2,1)S(1)} %copy-done.1, s32[64]{0:T(128)S(1)} %get-tuple-element.13, s32[64]{0:T(128)S(1)} %get-tuple-element.14, s32[64]{0:T(128)S(1)} %and_select_fusion.3), kind=kOutput, calls=%fused_computation.3 | convolution fusion | flops 1612787712 | bytes 20972288 | tf_op jit(solution)/shard_map/dot_general | solution.py:29
  467.7 22.5 %multiply_add_fusion = (f32[64,32768]{1,0:T(8,128)}, f32[64,32768]{1,0:T(8,128)}) fusion(f32[64,32768]{1,0:T(8,128)} %convolution_subtract_fusion, f32[64,32768]{1,0:T(8,128)} %convolution_subtract_fusion.1, f32[64,32768]{1,0:T(8,128)} %convolution_add_fusion, f32[64,32768]{1,0:T(8,128)} %fusion.28, bf16[8,8,256,128]{3,2,1,0:T(8,128)(2,1)} %get-tuple-element.11, ...), kind=kOutput, calls=%fused_computation.32 | convolution fusion | flops 1625370624 | bytes 54526720 | tf_op jit(solution)/shard_map/dot_general | solution.py:31
  490.2 12.3 %fusion.57 = f32[64,32768]{1,0:T(8,128)} fusion(f32[64,32768]{1,0:T(8,128)} %get-tuple-element.5, s32[64]{0:T(128)S(1)} %get-tuple-element.13, s32[64]{0:T(128)S(1)} %get-tuple-element.14, s32[64]{0:T(128)S(1)} %and_select_fusion.3), kind=kOutput, calls=%fused_computation.90 | convolution fusion | flops 1610690560 | bytes 16777984 | tf_op jit(solution)/shard_map/dot_general | solution.py:39
  502.6 7.8 fusion.58
  510.3 12.9 %fusion.44 = bf16[8,8,256,128]{3,1,2,0:T(8,128)(2,1)} fusion(f32[64,32768]{1,0:T(8,128)} %fusion.57, f32[64,32768]{1,0:T(8,128)S(1)} %copy-done, s32[64]{0:T(128)S(1)} %get-tuple-element.13, s32[64]{0:T(128)S(1)} %get-tuple-element.14, s32[64]{0:T(128)S(1)} %and_select_fusion.3), kind=kOutput, calls=%fused_computation.64 | convolution fusion | flops 1614884864 | bytes 20972288 | tf_op jit(solution)/shard_map/dot_general | solution.py:40
  523.3 10.8 fusion.45
  534.1 3.5 copy.20
  537.6 1.2 copy.21
  538.8 0.5 bitcast_dynamic-update-slice_fusion.1
  539.3 0.5 bitcast_dynamic-update-slice_fusion
  539.9 0.1 fusion.52
  540.0 0.1 fusion.51
  540.2 0.1 fusion.50
  540.3 0.1 fusion.49
  540.5 0.1 fusion.48
  540.9 186.6 %all_to_all.35 = bf16[8,2,8,256,128]{4,3,2,1,0:T(8,128)(2,1)S(1)} all-to-all(bf16[8,2,8,256,128]{4,3,2,1,0:T(8,128)(2,1)S(1)} %fusion.46), channel_id=1, replica_groups=mesh['kt'=8,'tile'=4] {'kt'}, dimensions={0} | all-to-all | bytes 16777216 | tf_op jit(solution)/shard_map/all_to_all | solution.py:83
  727.5 2.5 fusion.124
  730.0 4.8 copy.15
  734.9 7.3 squeeze.43
  742.1 6.9 copy.14
  749.0 7.4 squeeze.41
  756.5 15.1 %fusion.2 = f32[8,256,1024]{2,1,0:T(8,128)} fusion(bf16[8,256,1024]{2,1,0:T(8,128)(2,1)} %squeeze.41, bf16[2,8,1024,1024]{3,2,1,0:T(8,128)(2,1)} %param.5), kind=kOutput, calls=%fused_computation.11 | convolution fusion | flops 4294967296 | bytes 29360128 | tf_op jit(solution)/shard_map/kij,kjl->kil/dot_general | solution.py:59
  771.6 13.6 %fusion.4 = f32[8,256,1024]{2,1,0:T(8,128)} fusion(bf16[8,256,1024]{2,1,0:T(8,128)(2,1)S(1)} %copy-done.3, bf16[2,8,1024,1024]{3,2,1,0:T(8,128)(2,1)} %param.5), kind=kOutput, calls=%fused_computation.13 | convolution fusion | flops 4294967296 | bytes 29360128 | tf_op jit(solution)/shard_map/kij,kjl->kil/dot_general | solution.py:59
  785.2 14.7 %fusion.19 = bf16[1,8,256,1024]{3,2,1,0:T(8,128)(2,1)} fusion(f32[8,256,1024]{2,1,0:T(8,128)} %fusion.2, bf16[8,256,1024]{2,1,0:T(8,128)(2,1)S(1)} %copy-done.3, bf16[2,8,1024,1024]{3,2,1,0:T(8,128)(2,1)} %param.5), kind=kOutput, calls=%fused_computation.35 | convolution fusion | flops 4299161600 | bytes 33554432 | tf_op jit(solution)/shard_map/kij,kjl->kil/dot_general | solution.py:59
  799.9 13.7 %fusion.18 = bf16[1,8,256,1024]{3,2,1,0:T(8,128)(2,1)} fusion(f32[8,256,1024]{2,1,0:T(8,128)} %fusion.4, bf16[8,256,1024]{2,1,0:T(8,128)(2,1)} %squeeze.41, bf16[2,8,1024,1024]{3,2,1,0:T(8,128)(2,1)} %param.5), kind=kOutput, calls=%fused_computation.34 | convolution fusion | flops 4299161600 | bytes 33554432 | tf_op jit(solution)/shard_map/kij,kjl->kil/dot_general | solution.py:59
  813.7 6.4 pad_maximum_fusion
  820.1 200.7 %all-gather.2.cloned.1.call-done = bf16[2,8,1024,1024]{3,2,1,0:T(8,128)(2,1)} async-done(((bf16[2,8,256,1024]{3,2,1,0:T(8,128)(2,1)}), bf16[2,8,1024,1024]{3,2,1,0:T(8,128)(2,1)}) %all-gather.2.cloned.1.call-update) | async-done | bytes 33554448 | tf_op jit(solution)/shard_map/all_gather | solution.py:89
  1020.8 14.8 %fusion.11 = f32[8,256,1024]{2,1,0:T(8,128)} fusion(bf16[2,8,1024,1024]{3,2,1,0:T(8,128)(2,1)} %all-gather.2.cloned.1.call-done, bf16[2,8,1024,1024]{3,2,1,0:T(8,128)(2,1)} %param.5, s32[]{:T(128)S(6)} %select_n.170), kind=kOutput, calls=%fused_computation.20 | convolution fusion | flops 4294967296 | bytes 29360132 | tf_op jit(solution)/shard_map/kij,kjl->kil/dot_general | solution.py:59
  1035.6 15.0 %fusion.10 = f32[8,256,1024]{2,1,0:T(8,128)} fusion(bf16[2,8,1024,1024]{3,2,1,0:T(8,128)(2,1)} %all-gather.2.cloned.1.call-done, bf16[2,8,1024,1024]{3,2,1,0:T(8,128)(2,1)} %param.5, s32[]{:T(128)S(6)} %add.203, s32[]{:T(128)S(6)} %select_n.170), kind=kOutput, calls=%fused_computation.19 | convolution fusion | flops 4294967296 | bytes 29360136 | tf_op jit(solution)/shard_map/kij,kjl->kil/dot_general | solution.py:59
  1050.5 17.2 %add_bitcast_fusion = f32[1,8,256,1024]{3,2,1,0:T(8,128)} fusion(f32[8,256,1024]{2,1,0:T(8,128)} %fusion.10, bf16[2,8,1024,1024]{3,2,1,0:T(8,128)(2,1)} %all-gather.2.cloned.1.call-done, bf16[2,8,1024,1024]{3,2,1,0:T(8,128)(2,1)} %param.5, s32[]{:T(128)S(6)} %select_n.170), kind=kOutput, calls=%fused_computation.28 | convolution fusion | flops 4297064448 | bytes 37748740 | tf_op jit(solution)/shard_map/kij,kjl->kil/dot_general | solution.py:59
  1067.8 17.5 %subtract_bitcast_fusion = f32[1,8,256,1024]{3,2,1,0:T(8,128)} fusion(f32[8,256,1024]{2,1,0:T(8,128)} %fusion.11, bf16[2,8,1024,1024]{3,2,1,0:T(8,128)(2,1)} %all-gather.2.cloned.1.call-done, bf16[2,8,1024,1024]{3,2,1,0:T(8,128)(2,1)} %param.5, s32[]{:T(128)S(6)} %add.203, s32[]{:T(128)S(6)} %select_n.170), kind=kOutput, calls=%fused_computation.29 | convolution fusion | flops 4297064448 | bytes 37748744 | tf_op jit(solution)/shard_map/kij,kjl->kil/dot_general | solution.py:59
  1085.2 14.7 %maximum_add_fusion = f32[2,8,256,1024]{3,2,1,0:T(8,128)} fusion(f32[1,8,256,1024]{3,2,1,0:T(8,128)} %add_bitcast_fusion, f32[1,8,256,1024]{3,2,1,0:T(8,128)} %subtract_bitcast_fusion, bf16[2,8,1024,1024]{3,2,1,0:T(8,128)(2,1)} %param.5, s32[]{:T(128)S(6)} %select_n.170), kind=kLoop, calls=%fused_computation.10 | loop fusion | flops 12582912 | bytes 41943044 | tf_op jit(solution)/shard_map/add | solution.py:94
  (27 shorter events, 0.5 us)
Async XLA Ops:
  19.1 190.5 %all-to-all-start = ((bf16[2,8,256,1024]{2,1,0,3:T(8,128)(2,1)}), bf16[2,8,256,1024]{2,1,0,3:T(8,128)(2,1)}, u32[]{:S(2)}, u32[]{:S(2)}) async-start(bf16[2,8,256,1024]{2,1,0,3:T(8,128)(2,1)} %copy.10), calls=%async_computation | async-start | bytes 16777216 | tf_op jit(solution)/shard_map/all_to_all | solution.py:71
  209.6 187.3 %all-to-all-start.1 = ((bf16[2,8,256,1024]{2,1,0,3:T(8,128)(2,1)}), bf16[2,8,256,1024]{2,1,0,3:T(8,128)(2,1)}, u32[]{:S(2)}, u32[]{:S(2)}) async-start(bf16[2,8,256,1024]{2,1,0,3:T(8,128)(2,1)} %copy.12), calls=%async_computation.1 | async-start | bytes 16777216 | tf_op jit(solution)/shard_map/all_to_all | solution.py:72
  214.6 806.2 %all-gather.2.cloned.1.call-start = ((), (), s32[]{:S(2)}) async-start(), calls=%async_computation.3 | async-start | bytes 41943040 | tf_op jit(solution)/shard_map/all_gather | solution.py:89
  423.9 29.4 %slice-start.2 = ((s8[8388608]{0:T(1024)(128)(4,1)}), s8[4194304]{0:T(1024)(128)(4,1)S(1)}, s32[]{:S(2)}) async-start(s8[8388608]{0:T(1024)(128)(4,1)} %bitcast.143), calls=%async_computation.6 | async-start | bytes 8388608
  438.4 14.8 %copy-start.1 = (bf16[8,8,256,128]{3,2,1,0:T(8,128)(2,1)S(1)}, bf16[8,8,256,128]{3,2,1,0:T(8,128)(2,1)}, u32[]{:S(2)}) copy-start(bf16[8,8,256,128]{3,2,1,0:T(8,128)(2,1)} %get-tuple-element.11) | copy-start | bytes 12582916
  438.4 14.8 %slice-start.3 = ((s8[8388608]{0:T(1024)(128)(4,1)}), s8[4194304]{0:T(1024)(128)(4,1)S(1)}, s32[]{:S(2)}) async-start(s8[8388608]{0:T(1024)(128)(4,1)} %bitcast.143), calls=%async_computation.7 | async-start | bytes 8388608
  490.2 12.3 %copy-start = (f32[64,32768]{1,0:T(8,128)S(1)}, f32[64,32768]{1,0:T(8,128)}, u32[]{:S(2)}) copy-start(f32[64,32768]{1,0:T(8,128)} %get-tuple-element.6) | copy-start | bytes 25165828
  502.5 20.7 %slice-start = ((s8[8388608]{0:T(1024)(128)(4,1)}), s8[4194304]{0:T(1024)(128)(4,1)S(1)}, s32[]{:S(2)}) async-start(s8[8388608]{0:T(1024)(128)(4,1)} %bitcast.141), calls=%async_computation.4 | async-start | bytes 8388608
  510.3 12.9 %slice-start.1 = ((s8[8388608]{0:T(1024)(128)(4,1)}), s8[4194304]{0:T(1024)(128)(4,1)S(1)}, s32[]{:S(2)}) async-start(s8[8388608]{0:T(1024)(128)(4,1)} %bitcast.141), calls=%async_computation.5 | async-start | bytes 8388608
  534.1 3.5 copy-start.2
  756.5 15.1 %copy-start.3 = (bf16[8,256,1024]{2,1,0:T(8,128)(2,1)S(1)}, bf16[8,256,1024]{2,1,0:T(8,128)(2,1)}, u32[]{:S(2)}) copy-start(bf16[8,256,1024]{2,1,0:T(8,128)(2,1)} %squeeze.43) | copy-start | bytes 12582916
  799.9 13.8 %copy-start.4 = (bf16[1,8,256,1024]{3,2,1,0:T(8,128)(2,1)S(1)}, bf16[1,8,256,1024]{3,2,1,0:T(8,128)(2,1)}, u32[]{:S(2)}) copy-start(bf16[1,8,256,1024]{3,2,1,0:T(8,128)(2,1)} %fusion.19) | copy-start | bytes 12582916
Sparse Core Ops, SparseCore 0:
  820.2 200.5 all-gather.1
